TPU v7x, 32 devices: a whole 2x2x4 slice. The times are simulated.
32 devices in a mesh: ga: 8 (over z, core), gp: 4 (over y, x).
Axes of the slice: x: 2, y: 2, z: 4, core: 2. Of those that a mesh axis runs over, the one named last changes fastest.
Arguments:
- matel: bfloat16 [16, 16, 100352], P('ga', None, 'gp'), may hold values from -0.01953125 to 0.01953125
- pole_amp: bfloat16 [1024, 100352], P('ga', 'gp'), may hold values from -6 to 6
- pole_freq: bfloat16 [1024, 100352], P('ga', 'gp'), may hold values from 0.5 to 4
- band_energy: float32 [16], replicated, may hold values from -3 to 3
- energies: float32 [3], replicated, may hold values from -2 to 2
- owner: int32 [5], replicated, may hold values from 0 to 7
- slot: int32 [5], replicated, may hold values from 0 to 1
Outputs:
- sigma: float32 [3, 16, 16], replicated
Inputs may be any that keep to these rules, and one draw needn't show every extreme that they name: `slot`: position among the 2 bands stored by that row.
All inputs are finite; a program needn't handle non-finite values.
Results may differ from a plain program's by a relative error of at most 0.0029.
Values may be sent and summed in bfloat16 or wider, within the bound.
No kernel may reach another device: no remote copies, remote signals or barrier semaphores. Data moves between devices by JAX's collectives and lax.ppermute only.
A program may use at most 128 MiB of HBM per device.

v0:
```python
import jax
import jax.numpy as jnp
from jax import lax
from jax.sharding import PartitionSpec as P


def from_root(shard, axis, root):
    mine = lax.axis_index(axis) == root
    return lax.psum(jnp.where(mine, shard, jnp.zeros_like(shard)), axis)


def shards(matel, pole_amp, pole_freq, band_energy, energies, owner, slot):
    held_bands = matel.shape[0]
    states = matel.shape[1]
    cols_tile = matel.shape[2]
    rows_tile = pole_amp.shape[0]
    row_index = lax.axis_index("ga")
    first_row = row_index * rows_tile
    source = first_row // cols_tile
    offset = first_row % cols_tile
    amplitude = pole_amp.astype(jnp.float32)
    frequency = pole_freq.astype(jnp.float32)
    numerator = amplitude * frequency
    squared = frequency * frequency
    labels = jnp.arange(band_energy.shape[0], dtype=jnp.int32)
    partial_value = jnp.zeros((energies.shape[0], states, states), jnp.float32)
    for band_slot in range(owner.shape[0]):
        own_piece = lax.dynamic_index_in_dim(matel, slot[band_slot], 0, keepdims=False)
        column = from_root(own_piece, "ga", owner[band_slot])
        window_rows = lax.dynamic_slice_in_dim(column, offset, rows_tile, 1)
        row_piece = from_root(window_rows, "gp", source)
        band_level = jnp.sum(
            jnp.where(labels == owner[band_slot] * held_bands + slot[band_slot], band_energy, 0.0)
        )
        detuning = energies[:, None, None] - band_level
        pole_value = (numerator / (detuning * detuning + squared)).astype(jnp.bfloat16)
        folded = jnp.einsum("egk,sk->esg", pole_value, column, preferred_element_type=jnp.float32)
        partial_value = partial_value + jnp.einsum(
            "tg,esg->ets", row_piece.astype(jnp.float32), folded, precision=lax.Precision.HIGHEST
        )
    sigma_sum = lax.psum(partial_value, ("ga", "gp"))
    return sigma_sum


def solution(mesh):
    return jax.shard_map(
        shards,
        mesh=mesh,
        in_specs=(P("ga", None, "gp"), P("ga", "gp"), P("ga", "gp"), P(), P(), P(), P()),
        out_specs=P(),
        check_vma=False,
    )
```

profile of v0, /device:TPU:0, one launch (start us, length us, event | category | flops | bytes accessed | tf_op | source)
XLA Modules:
  0.0 232.1 jit_solution(8351332103755635350)
XLA Ops:
  6.5 0.0 all-reduce.4.cloned.1.call-start
  6.5 1.5 fusion.27
  14.1 1.5 fusion.28
  21.9 4.5 %select_bitcast_fusion = (bf16[16,25088]{1,0:T(8,128)(2,1)}, bf16[16,25088]{1,0:T(8,128)(2,1)}, bf16[16,25088]{1,0:T(8,128)(2,1)}, bf16[16,25088]{1,0:T(8,128)(2,1)}, bf16[16,25088]{1,0:T(8,128)(2,1)}) fusion(bf16[2,16,25088]{2,1,0:T(8,128)(2,1)} %param.7, s32[]{:T(128)S(6)} %select_n.150, pred[]{:T(512)S(6)} %eq.67, s32[]{:T(128)S(6)} %select_n.138, ...), kind=kLoop, calls=%fused_computation.27 | loop fusion | flops 2007040 | bytes 8028185 | tf_op jit(solution)/shard_map/jit(_where)/select_n | solution.py:9
  26.3 0.0 all-reduce.4.cloned.1.call-update
  26.4 0.0 copy-start.6
  26.4 0.0 copy-start.7
  26.4 12.5 %convert_multiply_fusion.1 = (f32[128,25088]{1,0:T(8,128)}, f32[128,25088]{1,0:T(8,128)}) fusion(bf16[128,25088]{1,0:T(8,128)(2,1)} %param.9, bf16[128,25088]{1,0:T(8,128)(2,1)} %param.8), kind=kLoop, calls=%fused_computation.11 | loop fusion | flops 12845056 | bytes 38535168 | tf_op jit(solution)/shard_map/mul | solution.py:23
  45.2 0.0 copy-done.6
  45.3 0.6 fusion.26
  45.9 0.0 copy-done.7
  45.9 3.6 %subtract_multiply_fusion = (f32[3]{0:T(128)S(1)}, f32[3]{0:T(128)S(1)}, f32[3]{0:T(128)S(1)}, f32[3]{0:T(128)}, f32[3]{0:T(128)S(1)}) fusion(f32[3]{0:T(128)S(1)} %copy-done.7, f32[]{:T(128)} %get-tuple-element.5, f32[]{:T(128)} %get-tuple-element.6, f32[]{:T(128)} %get-tuple-element.7, f32[]{:T(128)} %get-tuple-element.8, f32[]{:T(128)} %get-tuple-element.9), kind=kLoop, calls=%fused_computation.53 | loop fusion | flops 30 | bytes 92 | tf_op jit(solution)/shard_map/mul | solution.py:36
  49.5 73.6 %all-reduce.4.cloned.1.call-done = (bf16[16,25088]{1,0:T(8,128)(2,1)}, bf16[16,25088]{1,0:T(8,128)(2,1)}, bf16[16,25088]{1,0:T(8,128)(2,1)}, bf16[16,25088]{1,0:T(8,128)(2,1)}, bf16[16,25088]{1,0:T(8,128)(2,1)}) async-done(((bf16[16,25088]{1,0:T(8,128)(2,1)}, bf16[16,25088]{1,0:T(8,128)(2,1)}, bf16[16,25088]{1,0:T(8,128)(2,1)}, bf16[16,25088]{1,0:T(8,128)(2,1)}, bf16[16,25088]{1,0:T(8,128)(2,1)}), ...) | async-done | bytes 4014096 | tf_op jit(solution)/shard_map/psum | solution.py:9
  123.1 1.4 dynamic-slice_select_fusion.4
  124.5 1.4 dynamic-slice_select_fusion.2
  125.8 0.0 copy-start
  125.8 0.0 copy-start.1
  125.8 12.4 %fusion.8 = f32[3,16,128]{2,1,0:T(8,128)} fusion(f32[3]{0:T(128)S(1)} %get-tuple-element.29, f32[128,25088]{1,0:T(8,128)} %get-tuple-element.21, f32[128,25088]{1,0:T(8,128)} %get-tuple-element.20, bf16[16,25088]{1,0:T(8,128)(2,1)} %get-tuple-element.11), kind=kOutput, calls=%fused_computation.15 | convolution fusion | flops 337182720 | bytes 26517516 | tf_op jit(solution)/shard_map/egk,sk->esg/dot_general | solution.py:37
  138.3 0.0 copy-done
  138.3 3.5 %copy-done.1 = f32[128,25088]{1,0:T(8,128)S(1)} copy-done((f32[128,25088]{1,0:T(8,128)S(1)}, f32[128,25088]{1,0:T(8,128)}, u32[]{:S(2)}) %copy-start.1) | copy-done | bytes 12845080
  141.8 0.0 copy-start.9
  141.8 6.9 %fusion.7 = f32[3,16,128]{2,1,0:T(8,128)S(1)} fusion(f32[3]{0:T(128)S(1)} %get-tuple-element.28, f32[128,25088]{1,0:T(8,128)S(1)} %copy-done.1, f32[128,25088]{1,0:T(8,128)S(1)} %copy-done, bf16[16,25088]{1,0:T(8,128)(2,1)} %get-tuple-element.12), kind=kOutput, calls=%fused_computation.14 | convolution fusion | flops 337182720 | bytes 26517516 | tf_op jit(solution)/shard_map/egk,sk->esg/dot_general | solution.py:37
  148.7 0.0 copy-done.9
  148.7 0.8 dynamic-slice_select_fusion
  149.5 6.8 %fusion.6 = f32[3,16,128]{2,1,0:T(8,128)S(1)} fusion(f32[3]{0:T(128)S(1)} %get-tuple-element.31, f32[128,25088]{1,0:T(8,128)S(1)} %copy-done.1, f32[128,25088]{1,0:T(8,128)S(1)} %copy-done, bf16[16,25088]{1,0:T(8,128)(2,1)} %get-tuple-element.13), kind=kOutput, calls=%fused_computation.13 | convolution fusion | flops 337182720 | bytes 26517516 | tf_op jit(solution)/shard_map/egk,sk->esg/dot_general | solution.py:37
  156.3 0.0 copy-start.8
  156.3 5.2 %fusion.5 = f32[3,16,128]{2,1,0:T(8,128)S(1)} fusion(f32[3]{0:T(128)S(1)} %get-tuple-element.27, f32[128,25088]{1,0:T(8,128)S(1)} %copy-done.1, f32[128,25088]{1,0:T(8,128)S(1)} %copy-done, bf16[16,25088]{1,0:T(8,128)(2,1)S(1)} %copy-done.9), kind=kOutput, calls=%fused_computation.12 | convolution fusion | flops 337182720 | bytes 26517516 | tf_op jit(solution)/shard_map/egk,sk->esg/dot_general | solution.py:37
  161.5 0.0 copy-done.8
  161.5 0.0 copy-start.3
  161.5 0.0 copy-start.4
  161.5 0.0 copy-start.5
  161.5 0.0 copy-start.2
  161.5 6.8 %fusion.9 = f32[3,16,128]{2,1,0:T(8,128)S(1)} fusion(f32[128,25088]{1,0:T(8,128)S(1)} %copy-done.1, f32[3]{0:T(128)S(1)} %copy-done.8, f32[128,25088]{1,0:T(8,128)S(1)} %copy-done, bf16[16,25088]{1,0:T(8,128)(2,1)} %get-tuple-element.10), kind=kOutput, calls=%fused_computation.16 | convolution fusion | flops 337182720 | bytes 26517516 | tf_op jit(solution)/shard_map/egk,sk->esg/dot_general | solution.py:37
  168.4 0.0 copy-done.3
  168.4 0.0 copy-done.4
  168.4 0.0 copy-done.5
  168.4 16.2 %all-reduce.1 = (bf16[16,128]{1,0:T(8,128)(2,1)S(1)}, bf16[16,128]{1,0:T(8,128)(2,1)S(1)}, bf16[16,128]{1,0:T(8,128)(2,1)S(1)}, bf16[16,128]{1,0:T(8,128)(2,1)S(1)}, bf16[16,128]{1,0:T(8,128)(2,1)S(1)}) all-reduce(bf16[16,128]{1,0:T(8,128)(2,1)S(1)} %copy-done.5, ...), channel_id=1, replica_groups=mesh['ga'=8,'gp'=4] {'gp'}, use_global_device_ids=true, to_apply=%region_2.3 | all-reduce | flops 10240 | bytes 40960 | tf_op jit(solution)/shard_map/psum | solution.py:9
  184.6 0.1 fusion.20
  184.7 0.0 copy-done.2
  184.7 0.1 convolution_add_fusion.3
  184.8 0.1 convolution_add_fusion.2
  185.0 0.1 convolution_add_fusion.1
  185.1 0.1 fusion.10
  185.3 39.3 %psum.87 = f32[3,16,16]{1,2,0:T(8,128)S(1)} all-reduce(f32[3,16,16]{1,2,0:T(8,128)S(1)} %fusion.10), channel_id=1, replica_groups=mesh['ga'=8,'gp'=4] {'ga','gp'}, use_global_device_ids=true, to_apply=%region_15.16 | all-reduce | flops 768 | bytes 6144 | tf_op jit(solution)/shard_map/psum | solution.py:41
  224.5 0.7 copy.8
Async XLA Ops:
  6.5 116.5 %all-reduce.4.cloned.1.call-start = ((), (), s32[]{:S(2)}) async-start(), calls=%async_computation | async-start | bytes 8028160 | tf_op jit(solution)/shard_map/psum | solution.py:9
  26.4 18.9 %copy-start.6 = (f32[16]{0:T(128)S(1)}, f32[16]{0:T(128)}, u32[]{:S(2)}) copy-start(f32[16]{0:T(128)} %param.10) | copy-start | bytes 196
  26.4 19.5 %copy-start.7 = (f32[3]{0:T(128)S(1)}, f32[3]{0:T(128)}, u32[]{:S(2)}) copy-start(f32[3]{0:T(128)} %param.11) | copy-start | bytes 40
  125.8 12.4 %copy-start = (f32[128,25088]{1,0:T(8,128)S(1)}, f32[128,25088]{1,0:T(8,128)}, u32[]{:S(2)}) copy-start(f32[128,25088]{1,0:T(8,128)} %get-tuple-element.20) | copy-start | bytes 38535172
  125.8 15.9 %copy-start.1 = (f32[128,25088]{1,0:T(8,128)S(1)}, f32[128,25088]{1,0:T(8,128)}, u32[]{:S(2)}) copy-start(f32[128,25088]{1,0:T(8,128)} %get-tuple-element.21) | copy-start | bytes 38535172
  141.8 6.9 %copy-start.9 = (bf16[16,25088]{1,0:T(8,128)(2,1)S(1)}, bf16[16,25088]{1,0:T(8,128)(2,1)}, u32[]{:S(2)}) copy-start(bf16[16,25088]{1,0:T(8,128)(2,1)} %get-tuple-element.14) | copy-start | bytes 2408452
  156.3 5.2 %copy-start.8 = (f32[3]{0:T(128)S(1)}, f32[3]{0:T(128)}, u32[]{:S(2)}) copy-start(f32[3]{0:T(128)} %get-tuple-element.30) | copy-start | bytes 40
  161.5 6.9 %copy-start.3 = (bf16[16,128]{1,0:T(8,128)(2,1)S(1)}, bf16[16,128]{1,0:T(8,128)(2,1)}, u32[]{:S(2)}) copy-start(bf16[16,128]{1,0:T(8,128)(2,1)} %get-tuple-element.44) | copy-start | bytes 12292
  161.5 6.9 %copy-start.4 = (bf16[16,128]{1,0:T(8,128)(2,1)S(1)}, bf16[16,128]{1,0:T(8,128)(2,1)}, u32[]{:S(2)}) copy-start(bf16[16,128]{1,0:T(8,128)(2,1)} %get-tuple-element.45) | copy-start | bytes 12292
  161.5 6.9 %copy-start.5 = (bf16[16,128]{1,0:T(8,128)(2,1)S(1)}, bf16[16,128]{1,0:T(8,128)(2,1)}, u32[]{:S(2)}) copy-start(bf16[16,128]{1,0:T(8,128)(2,1)} %dynamic-slice_select_fusion.4) | copy-start | bytes 12292
  161.5 23.2 %copy-start.2 = (f32[3,16,128]{2,1,0:T(8,128)S(1)}, f32[3,16,128]{2,1,0:T(8,128)}, u32[]{:S(2)}) copy-start(f32[3,16,128]{2,1,0:T(8,128)} %fusion.8) | copy-start | bytes 73732
Sparse Core Ops, SparseCore 0:
  26.5 96.5 all-reduce.3
where the time goes:
time: 233 us; the launch traced here: 232 us
  waiting for transfers between devices  73.6 us (32%)
  blocking collectives  55.4 us (24%)
  matrix products  38.8 us (17%)
  between operations  32.2 us (14%)
  other arithmetic  24.8 us (11%)
  local copies, waits for them, and re-layouts  7.2 us (3%)
    psum x1, waiting for transfers between devices, from_root(): return lax.psum(jnp.where(mine, shard, jnp.zeros_like(shard)), axis)  73.6 us
    psum x1, blocking collectives, shards(): sigma_sum = lax.psum(partial_value, ('ga', 'gp'))  39.3 us
    dot_general x5, matrix products, shards(): jnp.einsum('egk,sk->esg', pole_value, column, preferred_element_type=jnp....  38.2 us
    psum x1, blocking collectives, from_root(): return lax.psum(jnp.where(mine, shard, jnp.zeros_like(shard)), axis)  16.2 us
    mul x1, other arithmetic, shards(): numerator = amplitude * frequency  12.5 us
    select_n x4, other arithmetic, from_root(): return lax.psum(jnp.where(mine, shard, jnp.zeros_like(shard)), axis)  8 us
  transfers between devices with their start and end apart: 1, of which 1 were waited for; matrix products, arithmetic and copies ran while one was open for 7% of the time, Pallas kernels for 0%

commit v1 on v0

--- a/solution.py
+++ b/solution.py
@@ -38,7 +38,9 @@
         partial_value = partial_value + jnp.einsum(
             "tg,esg->ets", row_piece.astype(jnp.float32), folded, precision=lax.Precision.HIGHEST
         )
-    sigma_sum = lax.psum(partial_value, ("ga", "gp"))
+    sigma_sum = partial_value
+    for mesh_axis in ("gp", "ga"):
+        sigma_sum = lax.psum(sigma_sum, mesh_axis)
     return sigma_sum
 
 

time: 233 us -> 234 us (level)
    psum x1 -> x2, blocking collectives: 39.3 us -> 40.2 us  [shards(): sigma_sum = lax.psum(sigma_sum, mesh_axis)]
where the time goes in v1:
time: 234 us; the launch traced here: 233 us
  waiting for transfers between devices  73.8 us (32%)
  blocking collectives  56.4 us (24%)
  matrix products  38.8 us (17%)
  between operations  31.9 us (14%)
  other arithmetic  24.8 us (11%)
  local copies, waits for them, and re-layouts  7.18 us (3%)
    psum x1, waiting for transfers between devices, from_root(): return lax.psum(jnp.where(mine, shard, jnp.zeros_like(shard)), axis)  73.7 us
    psum x2, blocking collectives, shards(): sigma_sum = lax.psum(sigma_sum, mesh_axis)  40.2 us
    dot_general x5, matrix products, shards(): jnp.einsum('egk,sk->esg', pole_value, column, preferred_element_type=jnp....  38.2 us
    psum x1, blocking collectives, from_root(): return lax.psum(jnp.where(mine, shard, jnp.zeros_like(shard)), axis)  16.2 us
    mul x1, other arithmetic, shards(): numerator = amplitude * frequency  12.5 us
    select_n x4, other arithmetic, from_root(): return lax.psum(jnp.where(mine, shard, jnp.zeros_like(shard)), axis)  8.02 us
  transfers between devices with their start and end apart: 1, of which 1 were waited for; matrix products, arithmetic and copies ran while one was open for 7% of the time, Pallas kernels for 0%

profile of v1, /device:TPU:0, one launch (start us, length us, event | category | flops | bytes accessed | tf_op | source)
XLA Modules:
  0.0 232.9 jit_solution(13836294585390810180)
XLA Ops:
  6.5 0.0 all-reduce.4.cloned.1.call-start
  6.5 1.4 fusion.27
  14.0 1.5 fusion.28
  21.7 4.5 %select_bitcast_fusion = (bf16[16,25088]{1,0:T(8,128)(2,1)}, bf16[16,25088]{1,0:T(8,128)(2,1)}, bf16[16,25088]{1,0:T(8,128)(2,1)}, bf16[16,25088]{1,0:T(8,128)(2,1)}, bf16[16,25088]{1,0:T(8,128)(2,1)}) fusion(bf16[2,16,25088]{2,1,0:T(8,128)(2,1)} %param.7, s32[]{:T(128)S(6)} %select_n.150, pred[]{:T(512)S(6)} %eq.67, s32[]{:T(128)S(6)} %select_n.138, ...), kind=kLoop, calls=%fused_computation.27 | loop fusion | flops 2007040 | bytes 8028185 | tf_op jit(solution)/shard_map/jit(_where)/select_n | solution.py:9
  26.2 0.0 all-reduce.4.cloned.1.call-update
  26.2 0.0 copy-start.6
  26.2 0.0 copy-start.7
  26.2 12.5 %convert_multiply_fusion.1 = (f32[128,25088]{1,0:T(8,128)}, f32[128,25088]{1,0:T(8,128)}) fusion(bf16[128,25088]{1,0:T(8,128)(2,1)} %param.9, bf16[128,25088]{1,0:T(8,128)(2,1)} %param.8), kind=kLoop, calls=%fused_computation.11 | loop fusion | flops 12845056 | bytes 38535168 | tf_op jit(solution)/shard_map/mul | solution.py:23
  44.9 0.0 copy-done.6
  45.0 0.6 fusion.26
  45.6 0.0 copy-done.7
  45.6 3.6 %subtract_multiply_fusion = (f32[3]{0:T(128)S(1)}, f32[3]{0:T(128)S(1)}, f32[3]{0:T(128)S(1)}, f32[3]{0:T(128)}, f32[3]{0:T(128)S(1)}) fusion(f32[3]{0:T(128)S(1)} %copy-done.7, f32[]{:T(128)} %get-tuple-element.5, f32[]{:T(128)} %get-tuple-element.6, f32[]{:T(128)} %get-tuple-element.7, f32[]{:T(128)} %get-tuple-element.8, f32[]{:T(128)} %get-tuple-element.9), kind=kLoop, calls=%fused_computation.53 | loop fusion | flops 30 | bytes 92 | tf_op jit(solution)/shard_map/mul | solution.py:36
  49.2 73.7 %all-reduce.4.cloned.1.call-done = (bf16[16,25088]{1,0:T(8,128)(2,1)}, bf16[16,25088]{1,0:T(8,128)(2,1)}, bf16[16,25088]{1,0:T(8,128)(2,1)}, bf16[16,25088]{1,0:T(8,128)(2,1)}, bf16[16,25088]{1,0:T(8,128)(2,1)}) async-done(((bf16[16,25088]{1,0:T(8,128)(2,1)}, bf16[16,25088]{1,0:T(8,128)(2,1)}, bf16[16,25088]{1,0:T(8,128)(2,1)}, bf16[16,25088]{1,0:T(8,128)(2,1)}, bf16[16,25088]{1,0:T(8,128)(2,1)}), ...) | async-done | bytes 4014096 | tf_op jit(solution)/shard_map/psum | solution.py:9
  122.9 1.4 dynamic-slice_select_fusion.4
  124.3 1.4 dynamic-slice_select_fusion.2
  125.7 0.0 copy-start
  125.7 0.0 copy-start.1
  125.7 12.4 %fusion.8 = f32[3,16,128]{2,1,0:T(8,128)} fusion(f32[3]{0:T(128)S(1)} %get-tuple-element.29, f32[128,25088]{1,0:T(8,128)} %get-tuple-element.21, f32[128,25088]{1,0:T(8,128)} %get-tuple-element.20, bf16[16,25088]{1,0:T(8,128)(2,1)} %get-tuple-element.11), kind=kOutput, calls=%fused_computation.15 | convolution fusion | flops 337182720 | bytes 26517516 | tf_op jit(solution)/shard_map/egk,sk->esg/dot_general | solution.py:37
  138.1 0.0 copy-done
  138.1 3.5 %copy-done.1 = f32[128,25088]{1,0:T(8,128)S(1)} copy-done((f32[128,25088]{1,0:T(8,128)S(1)}, f32[128,25088]{1,0:T(8,128)}, u32[]{:S(2)}) %copy-start.1) | copy-done | bytes 12845080
  141.6 0.0 copy-start.9
  141.6 6.9 %fusion.7 = f32[3,16,128]{2,1,0:T(8,128)S(1)} fusion(f32[3]{0:T(128)S(1)} %get-tuple-element.28, f32[128,25088]{1,0:T(8,128)S(1)} %copy-done.1, f32[128,25088]{1,0:T(8,128)S(1)} %copy-done, bf16[16,25088]{1,0:T(8,128)(2,1)} %get-tuple-element.12), kind=kOutput, calls=%fused_computation.14 | convolution fusion | flops 337182720 | bytes 26517516 | tf_op jit(solution)/shard_map/egk,sk->esg/dot_general | solution.py:37
  148.5 0.0 copy-done.9
  148.5 0.8 dynamic-slice_select_fusion
  149.3 6.8 %fusion.6 = f32[3,16,128]{2,1,0:T(8,128)S(1)} fusion(f32[3]{0:T(128)S(1)} %get-tuple-element.31, f32[128,25088]{1,0:T(8,128)S(1)} %copy-done.1, f32[128,25088]{1,0:T(8,128)S(1)} %copy-done, bf16[16,25088]{1,0:T(8,128)(2,1)} %get-tuple-element.13), kind=kOutput, calls=%fused_computation.13 | convolution fusion | flops 337182720 | bytes 26517516 | tf_op jit(solution)/shard_map/egk,sk->esg/dot_general | solution.py:37
  156.1 0.0 copy-start.8
  156.1 5.2 %fusion.5 = f32[3,16,128]{2,1,0:T(8,128)S(1)} fusion(f32[3]{0:T(128)S(1)} %get-tuple-element.27, f32[128,25088]{1,0:T(8,128)S(1)} %copy-done.1, f32[128,25088]{1,0:T(8,128)S(1)} %copy-done, bf16[16,25088]{1,0:T(8,128)(2,1)S(1)} %copy-done.9), kind=kOutput, calls=%fused_computation.12 | convolution fusion | flops 337182720 | bytes 26517516 | tf_op jit(solution)/shard_map/egk,sk->esg/dot_general | solution.py:37
  161.3 0.0 copy-done.8
  161.3 0.0 copy-start.3
  161.3 0.0 copy-start.4
  161.3 0.0 copy-start.5
  161.4 0.0 copy-start.2
  161.4 6.8 %fusion.9 = f32[3,16,128]{2,1,0:T(8,128)S(1)} fusion(f32[128,25088]{1,0:T(8,128)S(1)} %copy-done.1, f32[3]{0:T(128)S(1)} %copy-done.8, f32[128,25088]{1,0:T(8,128)S(1)} %copy-done, bf16[16,25088]{1,0:T(8,128)(2,1)} %get-tuple-element.10), kind=kOutput, calls=%fused_computation.16 | convolution fusion | flops 337182720 | bytes 26517516 | tf_op jit(solution)/shard_map/egk,sk->esg/dot_general | solution.py:37
  168.2 0.0 copy-done.3
  168.2 0.0 copy-done.4
  168.2 0.0 copy-done.5
  168.2 16.2 %all-reduce.1 = (bf16[16,128]{1,0:T(8,128)(2,1)S(1)}, bf16[16,128]{1,0:T(8,128)(2,1)S(1)}, bf16[16,128]{1,0:T(8,128)(2,1)S(1)}, bf16[16,128]{1,0:T(8,128)(2,1)S(1)}, bf16[16,128]{1,0:T(8,128)(2,1)S(1)}) all-reduce(bf16[16,128]{1,0:T(8,128)(2,1)S(1)} %copy-done.5, ...), channel_id=1, replica_groups=mesh['ga'=8,'gp'=4] {'gp'}, use_global_device_ids=true, to_apply=%region_2.3 | all-reduce | flops 10240 | bytes 40960 | tf_op jit(solution)/shard_map/psum | solution.py:9
  184.4 0.1 fusion.20
  184.5 0.0 copy-done.2
  184.5 0.1 convolution_add_fusion.3
  184.7 0.1 convolution_add_fusion.2
  184.8 0.1 convolution_add_fusion.1
  185.0 0.1 fusion.10
  185.1 14.3 %psum.94 = f32[3,16,16]{1,2,0:T(8,128)S(1)} all-reduce(f32[3,16,16]{1,2,0:T(8,128)S(1)} %fusion.10), channel_id=1, replica_groups=mesh['ga'=8,'gp'=4] {'gp'}, use_global_device_ids=true, to_apply=%region_15.16 | all-reduce | flops 768 | bytes 6144 | tf_op jit(solution)/shard_map/psum | solution.py:43
  199.4 26.0 %psum.95 = f32[3,16,16]{1,2,0:T(8,128)S(1)} all-reduce(f32[3,16,16]{1,2,0:T(8,128)S(1)} %psum.94), channel_id=1, replica_groups=mesh['ga'=8,'gp'=4] {'ga'}, use_global_device_ids=true, to_apply=%region_16.17 | all-reduce | flops 768 | bytes 6144 | tf_op jit(solution)/shard_map/psum | solution.py:43
  225.3 0.7 copy.8
Async XLA Ops:
  6.5 116.4 %all-reduce.4.cloned.1.call-start = ((), (), s32[]{:S(2)}) async-start(), calls=%async_computation | async-start | bytes 8028160 | tf_op jit(solution)/shard_map/psum | solution.py:9
  26.2 18.8 %copy-start.6 = (f32[16]{0:T(128)S(1)}, f32[16]{0:T(128)}, u32[]{:S(2)}) copy-start(f32[16]{0:T(128)} %param.10) | copy-start | bytes 196
  26.2 19.4 %copy-start.7 = (f32[3]{0:T(128)S(1)}, f32[3]{0:T(128)}, u32[]{:S(2)}) copy-start(f32[3]{0:T(128)} %param.11) | copy-start | bytes 40
  125.7 12.4 %copy-start = (f32[128,25088]{1,0:T(8,128)S(1)}, f32[128,25088]{1,0:T(8,128)}, u32[]{:S(2)}) copy-start(f32[128,25088]{1,0:T(8,128)} %get-tuple-element.20) | copy-start | bytes 38535172
  125.7 15.9 %copy-start.1 = (f32[128,25088]{1,0:T(8,128)S(1)}, f32[128,25088]{1,0:T(8,128)}, u32[]{:S(2)}) copy-start(f32[128,25088]{1,0:T(8,128)} %get-tuple-element.21) | copy-start | bytes 38535172
  141.6 6.9 %copy-start.9 = (bf16[16,25088]{1,0:T(8,128)(2,1)S(1)}, bf16[16,25088]{1,0:T(8,128)(2,1)}, u32[]{:S(2)}) copy-start(bf16[16,25088]{1,0:T(8,128)(2,1)} %get-tuple-element.14) | copy-start | bytes 2408452
  156.1 5.2 %copy-start.8 = (f32[3]{0:T(128)S(1)}, f32[3]{0:T(128)}, u32[]{:S(2)}) copy-start(f32[3]{0:T(128)} %get-tuple-element.30) | copy-start | bytes 40
  161.3 6.9 %copy-start.3 = (bf16[16,128]{1,0:T(8,128)(2,1)S(1)}, bf16[16,128]{1,0:T(8,128)(2,1)}, u32[]{:S(2)}) copy-start(bf16[16,128]{1,0:T(8,128)(2,1)} %get-tuple-element.44) | copy-start | bytes 12292
  161.3 6.9 %copy-start.4 = (bf16[16,128]{1,0:T(8,128)(2,1)S(1)}, bf16[16,128]{1,0:T(8,128)(2,1)}, u32[]{:S(2)}) copy-start(bf16[16,128]{1,0:T(8,128)(2,1)} %get-tuple-element.45) | copy-start | bytes 12292
  161.3 6.9 %copy-start.5 = (bf16[16,128]{1,0:T(8,128)(2,1)S(1)}, bf16[16,128]{1,0:T(8,128)(2,1)}, u32[]{:S(2)}) copy-start(bf16[16,128]{1,0:T(8,128)(2,1)} %dynamic-slice_select_fusion.4) | copy-start | bytes 12292
  161.4 23.2 %copy-start.2 = (f32[3,16,128]{2,1,0:T(8,128)S(1)}, f32[3,16,128]{2,1,0:T(8,128)}, u32[]{:S(2)}) copy-start(f32[3,16,128]{2,1,0:T(8,128)} %fusion.8) | copy-start | bytes 73732
Sparse Core Ops, SparseCore 0:
  26.3 96.5 all-reduce.3
